TPU v7x, 32 devices: a whole 2x2x4 slice. The times are simulated.
32 devices in a mesh: dp: 8 (over z, y), tensor: 4 (over x, core).
Axes of the slice: x: 2, y: 2, z: 4, core: 2. Of those that a mesh axis runs over, the one named last changes fastest.
Arguments:
- layer_input: bfloat16 [3072, 2304], P('dp'), may hold values from -6 to 6
- cotangent: bfloat16 [3072, 2304], P('dp'), may hold values from -6 to 6
- seq_lengths: int32 [8, 8], P('dp'), may hold values from 0 to 256, as said below
- norm_attn_in: float32 [2304], replicated, may hold values from 0.1 to 1.9
- w_query: bfloat16 [2304, 2048], P('dp', 'tensor'), may hold values from -1 to 1
- w_key: bfloat16 [2304, 1024], P('dp', 'tensor'), may hold values from -1 to 1
- w_value: bfloat16 [2304, 1024], P('dp', 'tensor'), may hold values from -0.125 to 0.125
- w_out: bfloat16 [2048, 2304], P('tensor', 'dp'), may hold values from -0.125 to 0.125
- norm_attn_out: float32 [2304], replicated, may hold values from 0.1 to 1.9
- norm_ffn_in: float32 [2304], replicated, may hold values from 0.1 to 1.9
- w_gate: bfloat16 [2304, 9216], P('dp', 'tensor'), may hold values from -0.125 to 0.125
- w_up: bfloat16 [2304, 9216], P('dp', 'tensor'), may hold values from -0.125 to 0.125
- w_down: bfloat16 [9216, 2304], P('tensor', 'dp'), may hold values from -0.0625 to 0.0625
- norm_ffn_out: float32 [2304], replicated, may hold values from 0.1 to 1.9
Outputs:
- layer_output: bfloat16 [3072, 2304], P('dp')
- input_grad: float32 [3072, 2304], P('dp')
- grad_norm_attn_in: float32 [2304], P('dp')
- grad_w_query: float32 [2304, 2048], P('dp', 'tensor')
- grad_w_key: float32 [2304, 1024], P('dp', 'tensor')
- grad_w_value: float32 [2304, 1024], P('dp', 'tensor')
- grad_w_out: float32 [2048, 2304], P('tensor', 'dp')
- grad_norm_attn_out: float32 [2304], P('dp')
- grad_norm_ffn_in: float32 [2304], P('dp')
- grad_w_gate: float32 [2304, 9216], P('dp', 'tensor')
- grad_w_up: float32 [2304, 9216], P('dp', 'tensor')
- grad_w_down: float32 [9216, 2304], P('tensor', 'dp')
- grad_norm_ffn_out: float32 [2304], P('dp')
Inputs may be any that keep to these rules, and one draw needn't show every extreme that they name: `seq_lengths`: row r lists the lengths of the sequences on data index r in packing order; slots after the last sequence hold 0. Each row sums to at most 384 and some row sums to exactly 384; some sequence has exactly 256 tokens.
All inputs are finite; a program needn't handle non-finite values.
Results may differ from a plain program's by a relative error of at most 0.02.
The roundings to bfloat16 on the way count: a program that leaves them out, or rounds other values in their place, can miss the bound.
Values may be sent and summed in bfloat16 or wider, within the bound.
A program may use at most 256 MiB of HBM per device.

v0:
```python
import math
import jax
import jax.numpy as jnp
from jax import lax
from jax.sharding import PartitionSpec as P

H = 8
KV = 4
HD = 256
EPSILON = 1e-06
SOFT_CAP = 50.0
QUERY_SCALE = 0.0625
GELU_COEFF = 0.7978845608028654


def rms_scale(values, scales):
    return values * lax.rsqrt(jnp.mean(values * values, axis=-1, keepdims=True) + EPSILON) * scales


def gelu_tanh(inputs):
    return (
        0.5 * inputs * (1.0 + jnp.tanh(GELU_COEFF * (inputs + 0.044715 * inputs * inputs * inputs)))
    )


def rotate_half(heads):
    middle = heads.shape[-1] // 2
    return jnp.concatenate([-heads[..., middle:], heads[..., :middle]], axis=-1)


def layout(lengths, row_count):
    seq_ends = jnp.cumsum(lengths)
    row_index = jnp.arange(row_count, dtype=jnp.int32)
    passed = (row_index[:, None] >= seq_ends[None, :]).astype(jnp.int32)
    segment = jnp.sum(passed, axis=1)
    is_live = row_index < seq_ends[-1]
    seq_ident = jnp.where(is_live, segment, lengths.shape[0] + row_index)
    offset = row_index - jnp.sum(passed * lengths[None, :], axis=1)
    allowed = (seq_ident[:, None] == seq_ident[None, :]) & (
        row_index[None, :] <= row_index[:, None]
    )
    middle = HD // 2
    inverse = jnp.exp(jnp.arange(middle, dtype=jnp.float32) * (-2.0 * math.log(10000.0) / HD))
    angles = offset.astype(jnp.float32)[:, None] * inverse[None, :]
    cosine = jnp.concatenate([jnp.cos(angles), jnp.cos(angles)], axis=1)
    sine_wave = jnp.concatenate([jnp.sin(angles), jnp.sin(angles)], axis=1)
    return (is_live, allowed, cosine, sine_wave)


def matmul(left, right):
    return jnp.dot(left, right, preferred_element_type=jnp.float32)


def left_product(left, right):
    return jnp.einsum("td,tc->dc", left, right, preferred_element_type=jnp.float32)


def right_product(left, right):
    return jnp.einsum("tc,dc->td", left, right, preferred_element_type=jnp.float32)


def capped_scores(query, keys):
    raw_scores = jnp.einsum("kgqd,ksd->kgqs", query, keys, preferred_element_type=jnp.float32)
    return SOFT_CAP * jnp.tanh(raw_scores / SOFT_CAP)


def shards(
    layer_input,
    cotangent,
    seq_lengths,
    norm_attn_in,
    w_query,
    w_key,
    w_value,
    w_out,
    norm_attn_out,
    norm_ffn_in,
    w_gate,
    w_up,
    w_down,
    norm_ffn_out,
):
    gathered = (
        lax.all_gather(w_query, "dp", axis=0, tiled=True),
        lax.all_gather(w_key, "dp", axis=0, tiled=True),
        lax.all_gather(w_value, "dp", axis=0, tiled=True),
        lax.all_gather(w_out, "dp", axis=1, tiled=True),
        lax.all_gather(w_gate, "dp", axis=0, tiled=True),
        lax.all_gather(w_up, "dp", axis=0, tiled=True),
        lax.all_gather(w_down, "dp", axis=1, tiled=True),
    )
    query_full, key_full, value_full, out_full, gate_full, up_full, down_full = gathered
    row_count = layer_input.shape[0]
    is_live, allowed, cosine, sine_wave = layout(seq_lengths[0], row_count)
    kv_heads = key_full.shape[1] // HD
    groups = H // KV
    layer_float = layer_input.astype(jnp.float32)
    h_attn = rms_scale(layer_float, norm_attn_in).astype(jnp.bfloat16)
    query_pre = (
        matmul(h_attn, query_full).reshape(row_count, kv_heads, groups, HD).transpose(1, 2, 0, 3)
    )
    query = ((query_pre * cosine + rotate_half(query_pre) * sine_wave) * QUERY_SCALE).astype(
        jnp.bfloat16
    )
    key_pre = matmul(h_attn, key_full).reshape(row_count, kv_heads, HD).transpose(1, 0, 2)
    keys = (key_pre * cosine + rotate_half(key_pre) * sine_wave).astype(jnp.bfloat16)
    values = (
        matmul(h_attn, value_full)
        .astype(jnp.bfloat16)
        .reshape(row_count, kv_heads, HD)
        .transpose(1, 0, 2)
    )
    capped = capped_scores(query, keys)
    expo = jnp.where(allowed, jnp.exp(capped), 0.0)
    log_total = jnp.log(jnp.sum(expo, axis=-1, keepdims=True))
    probs = jnp.where(allowed, jnp.exp(capped - log_total), 0.0).astype(jnp.bfloat16)
    mixed = jnp.einsum("kgqs,ksd->kgqd", probs, values, preferred_element_type=jnp.float32).astype(
        jnp.bfloat16
    )
    mixed_flat = mixed.transpose(2, 0, 1, 3).reshape(row_count, -1)
    attn_branch = lax.psum(matmul(mixed_flat, out_full), "tensor")
    resid = layer_float + rms_scale(attn_branch, norm_attn_out)
    h_ffn = rms_scale(resid, norm_ffn_in).astype(jnp.bfloat16)
    gate_pre = matmul(h_ffn, gate_full)
    up_pre = matmul(h_ffn, up_full)
    gelu_gate = gelu_tanh(gate_pre)
    hidden = (gelu_gate * up_pre).astype(jnp.bfloat16)
    ffn_branch = lax.psum(matmul(hidden, down_full), "tensor")
    layer_output = (resid + rms_scale(ffn_branch, norm_ffn_out)).astype(jnp.bfloat16)
    query_back, key_back, value_back, out_back, gate_back, up_back, down_back = gathered
    grad_out = cotangent.astype(jnp.float32) * is_live[:, None].astype(jnp.float32)
    _, pull_four = jax.vjp(rms_scale, ffn_branch, norm_ffn_out)
    grad_ffn_float, grad_norm_ffn_out = pull_four(grad_out)
    grad_ffn_branch = grad_ffn_float.astype(jnp.bfloat16)
    grad_w_down = left_product(hidden, grad_ffn_branch)
    grad_hidden = right_product(grad_ffn_branch, down_back)
    grad_up = (grad_hidden * gelu_gate).astype(jnp.bfloat16)
    _, pull_gelu = jax.vjp(gelu_tanh, gate_pre)
    grad_gate = pull_gelu(grad_hidden * up_pre)[0].astype(jnp.bfloat16)
    grad_w_gate = left_product(h_ffn, grad_gate)
    grad_w_up = left_product(h_ffn, grad_up)
    grad_h_ffn = lax.psum(
        right_product(grad_gate, gate_back) + right_product(grad_up, up_back), "tensor"
    )
    _, pull_three = jax.vjp(rms_scale, resid, norm_ffn_in)
    grad_resid_part, grad_norm_ffn_in = pull_three(grad_h_ffn)
    grad_resid = grad_out + grad_resid_part
    _, pull_two = jax.vjp(rms_scale, attn_branch, norm_attn_out)
    grad_attn_float, grad_norm_attn_out = pull_two(grad_resid)
    grad_attn_branch = grad_attn_float.astype(jnp.bfloat16)
    grad_w_out = left_product(mixed_flat, grad_attn_branch)
    grad_mixed = right_product(grad_attn_branch, out_back).astype(jnp.bfloat16)
    grad_mixed = grad_mixed.reshape(row_count, kv_heads, groups, HD).transpose(1, 2, 0, 3)
    capped_back = capped_scores(query, keys)
    weights_back = jnp.where(allowed, jnp.exp(capped_back - log_total), 0.0)
    grad_values = jnp.einsum(
        "kgqs,kgqd->ksd",
        weights_back.astype(jnp.bfloat16),
        grad_mixed,
        preferred_element_type=jnp.float32,
    ).astype(jnp.bfloat16)
    grad_probs = jnp.einsum(
        "kgqd,ksd->kgqs", grad_mixed, values, preferred_element_type=jnp.float32
    )
    row_delta = jnp.sum(weights_back * grad_probs, axis=-1, keepdims=True)
    tanh_part = capped_back / SOFT_CAP
    grad_scores = (weights_back * (grad_probs - row_delta) * (1.0 - tanh_part * tanh_part)).astype(
        jnp.bfloat16
    )
    grad_query_raw = jnp.einsum(
        "kgqs,ksd->kgqd", grad_scores, keys, preferred_element_type=jnp.float32
    )
    grad_query = (
        (grad_query_raw * cosine - rotate_half(grad_query_raw) * sine_wave) * QUERY_SCALE
    ).astype(jnp.bfloat16)
    grad_keys_raw = jnp.einsum(
        "kgqs,kgqd->ksd", grad_scores, query, preferred_element_type=jnp.float32
    )
    grad_keys = (grad_keys_raw * cosine - rotate_half(grad_keys_raw) * sine_wave).astype(
        jnp.bfloat16
    )
    grad_query_flat = grad_query.transpose(2, 0, 1, 3).reshape(row_count, -1)
    grad_keys_flat = grad_keys.transpose(1, 0, 2).reshape(row_count, -1)
    grad_values_flat = grad_values.transpose(1, 0, 2).reshape(row_count, -1)
    grad_w_query = left_product(h_attn, grad_query_flat)
    grad_w_key = left_product(h_attn, grad_keys_flat)
    grad_w_value = left_product(h_attn, grad_values_flat)
    local_h_attn = (
        right_product(grad_query_flat, query_back)
        + right_product(grad_keys_flat, key_back)
        + right_product(grad_values_flat, value_back)
    )
    grad_h_attn = lax.psum(local_h_attn.astype(jnp.bfloat16), "tensor").astype(jnp.float32)
    _, pull_one = jax.vjp(rms_scale, layer_float, norm_attn_in)
    grad_input_part, grad_norm_attn_in = pull_one(grad_h_attn)
    input_grad = grad_resid + grad_input_part
    summed = (
        lax.psum_scatter(
            grad_norm_attn_in.astype(jnp.bfloat16), "dp", scatter_dimension=0, tiled=True
        ).astype(jnp.float32),
        lax.psum_scatter(
            grad_w_query.astype(jnp.bfloat16), "dp", scatter_dimension=0, tiled=True
        ).astype(jnp.float32),
        lax.psum_scatter(
            grad_w_key.astype(jnp.bfloat16), "dp", scatter_dimension=0, tiled=True
        ).astype(jnp.float32),
        lax.psum_scatter(
            grad_w_value.astype(jnp.bfloat16), "dp", scatter_dimension=0, tiled=True
        ).astype(jnp.float32),
        lax.psum_scatter(
            grad_w_out.astype(jnp.bfloat16), "dp", scatter_dimension=1, tiled=True
        ).astype(jnp.float32),
        lax.psum_scatter(
            grad_norm_attn_out.astype(jnp.bfloat16), "dp", scatter_dimension=0, tiled=True
        ).astype(jnp.float32),
        lax.psum_scatter(
            grad_norm_ffn_in.astype(jnp.bfloat16), "dp", scatter_dimension=0, tiled=True
        ).astype(jnp.float32),
        lax.psum_scatter(
            grad_w_gate.astype(jnp.bfloat16), "dp", scatter_dimension=0, tiled=True
        ).astype(jnp.float32),
        lax.psum_scatter(
            grad_w_up.astype(jnp.bfloat16), "dp", scatter_dimension=0, tiled=True
        ).astype(jnp.float32),
        lax.psum_scatter(
            grad_w_down.astype(jnp.bfloat16), "dp", scatter_dimension=1, tiled=True
        ).astype(jnp.float32),
        lax.psum_scatter(
            grad_norm_ffn_out.astype(jnp.bfloat16), "dp", scatter_dimension=0, tiled=True
        ).astype(jnp.float32),
    )
    (
        sum_attn_in,
        sum_query,
        sum_key,
        sum_value,
        sum_out,
        sum_attn_out,
        sum_ffn_in,
        sum_gate,
        sum_up,
        sum_down,
        sum_ffn_out,
    ) = summed
    return (
        layer_output,
        input_grad,
        sum_attn_in,
        sum_query,
        sum_key,
        sum_value,
        sum_out,
        sum_attn_out,
        sum_ffn_in,
        sum_gate,
        sum_up,
        sum_down,
        sum_ffn_out,
    )


def solution(mesh):
    placed = (
        P("dp", None),
        P("dp", None),
        P("dp", None),
        P(),
        P("dp", "tensor"),
        P("dp", "tensor"),
        P("dp", "tensor"),
        P("tensor", "dp"),
        P(),
        P(),
        P("dp", "tensor"),
        P("dp", "tensor"),
        P("tensor", "dp"),
        P(),
    )
    return jax.shard_map(
        shards,
        mesh=mesh,
        in_specs=placed,
        out_specs=(
            P("dp", None),
            P("dp", None),
            P("dp"),
            P("dp", "tensor"),
            P("dp", "tensor"),
            P("dp", "tensor"),
            P("tensor", "dp"),
            P("dp"),
            P("dp"),
            P("dp", "tensor"),
            P("dp", "tensor"),
            P("tensor", "dp"),
            P("dp"),
        ),
        check_vma=False,
    )
```

profile of v0, /device:TPU:0, one launch (start us, length us, event | category | flops | bytes accessed | tf_op | source)
XLA Modules:
  0.0 1854.5 jit_solution(15311761673181839978)
XLA Ops:
  12.2 1.9 fusion.17
  15.7 38.3 %all-gather.10.cloned.1.call-done = bf16[2304,256]{1,0:T(8,128)(2,1)} async-done(((bf16[288,256]{1,0:T(8,128)(2,1)}), bf16[2304,256]{1,0:T(8,128)(2,1)}) %all-gather.10.cloned.1.call-update) | async-done | bytes 1179664 | tf_op jit(solution)/shard_map/all_gather | solution.py:85
  54.0 2.7 fusion.94
  57.0 39.1 %all-gather.12.cloned.1.call-done = bf16[2304,256]{1,0:T(8,128)(2,1)} async-done(((bf16[288,256]{1,0:T(8,128)(2,1)}), bf16[2304,256]{1,0:T(8,128)(2,1)}) %all-gather.12.cloned.1.call-update) | async-done | bytes 1179664 | tf_op jit(solution)/shard_map/all_gather | solution.py:86
  96.1 1.9 fusion.31
  98.0 50.8 %all-gather.8.cloned.1.call-done = bf16[2304,512]{1,0:T(8,128)(2,1)} async-done(((bf16[288,512]{1,0:T(8,128)(2,1)}), bf16[2304,512]{1,0:T(8,128)(2,1)}) %all-gather.8.cloned.1.call-update) | async-done | bytes 2359312 | tf_op jit(solution)/shard_map/all_gather | solution.py:84
  148.8 3.2 fusion.96
  154.2 47.0 %all-gather.14.cloned.1.call-done = bf16[512,2304]{0,1:T(8,128)(2,1)} async-done(((bf16[512,288]{0,1:T(8,128)(2,1)}), bf16[512,2304]{0,1:T(8,128)(2,1)}) %all-gather.14.cloned.1.call-update) | async-done | bytes 2359312 | tf_op jit(solution)/shard_map/all_gather | solution.py:87
  201.2 4.6 fusion.99
  208.1 71.2 %all-reduce.10.cloned.1.call-done = f32[384,2304]{1,0:T(8,128)} async-done(((f32[384,2304]{1,0:T(8,128)}), f32[384,2304]{1,0:T(8,128)}) %all-reduce.10.cloned.1.call-update) | async-done | bytes 3538960 | tf_op jit(solution)/shard_map/psum | solution.py:121
  279.4 2.5 multiply_reduce_fusion.8
  282.4 2.3 multiply_reduce_fusion.7
  285.9 1.6 multiply_convert_fusion.2
  287.5 146.2 %all-gather.16.cloned.1.call-done = bf16[2304,2304]{1,0:T(8,128)(2,1)} async-done(((bf16[288,2304]{1,0:T(8,128)(2,1)}), bf16[2304,2304]{1,0:T(8,128)(2,1)}) %all-gather.16.cloned.1.call-update) | async-done | bytes 10616848 | tf_op jit(solution)/shard_map/all_gather | solution.py:88
  433.7 10.6 fusion.100
  444.3 141.9 %all-gather.18.cloned.1.call-done = bf16[2304,2304]{1,0:T(8,128)(2,1)} async-done(((bf16[288,2304]{1,0:T(8,128)(2,1)}), bf16[2304,2304]{1,0:T(8,128)(2,1)}) %all-gather.18.cloned.1.call-update) | async-done | bytes 10616848 | tf_op jit(solution)/shard_map/all_gather | solution.py:89
  586.2 12.3 multiply_convert_fusion.1
  598.5 140.2 %all-gather.20.cloned.1.call-done = bf16[2304,2304]{0,1:T(8,128)(2,1)} async-done(((bf16[2304,288]{0,1:T(8,128)(2,1)}), bf16[2304,2304]{0,1:T(8,128)(2,1)}) %all-gather.20.cloned.1.call-update) | async-done | bytes 10616848 | tf_op jit(solution)/shard_map/all_gather | solution.py:90
  738.7 10.6 fusion.101
  750.8 71.7 %all-reduce.12.cloned.1.call-done = f32[384,2304]{1,0:T(8,128)} async-done(((f32[384,2304]{1,0:T(8,128)}), f32[384,2304]{1,0:T(8,128)}) %all-reduce.12.cloned.1.call-update) | async-done | bytes 3538960 | tf_op jit(solution)/shard_map/psum | solution.py:128
  822.5 2.5 multiply_reduce_fusion.6
  825.6 5.0 multiply_reduce_fusion
  830.6 13.1 multiply_convert_fusion
  843.8 7.7 fusion.102
  851.5 12.9 convolution_add_fusion.2
  865.0 3.5 fusion.24
  868.4 71.1 %all-reduce.14.cloned.1.call-done = f32[384,2304]{1,0:T(8,128)} async-done(((f32[384,2304]{1,0:T(8,128)}), f32[384,2304]{1,0:T(8,128)}) %all-reduce.14.cloned.1.call-update) | async-done | bytes 3538960 | tf_op jit(solution)/shard_map/psum | solution.py:142
  939.6 3.7 multiply_reduce_fusion.1
  943.8 4.1 multiply_reduce_fusion.2
  949.7 1.3 copy-done.21
  952.6 1.4 fusion.59
  954.0 3.3 fusion.37
  957.3 3.3 fusion.34
  960.6 2.6 fusion.30
  967.4 1.9 fusion.4
  969.4 2.0 convolution_convert_fusion.6
  971.5 2.0 convolution_convert_fusion.5
  973.7 3.0 convolution_convert_fusion.4
  976.8 4.4 convolution_convert_fusion.3
  981.3 9.9 convolution_convert_fusion.2
  991.3 1.4 copy-done.57
  992.7 8.3 convolution_convert_fusion.1
  1001.2 1.8 copy-done.8
  1003.0 10.7 convolution_convert_fusion
  1013.7 1.4 dynamic-slice
  1015.8 3.9 fusion.6
  1019.7 38.6 %all-reduce.4 = (bf16[2304]{0:T(1024)(128)(2,1)}, bf16[2304]{0:T(1024)(128)(2,1)}, bf16[2304]{0:T(1024)(128)(2,1)}, bf16[2304]{0:T(1024)(128)(2,1)}) all-reduce(bf16[2304]{0:T(1024)(128)(2,1)} %get-tuple-element.19, bf16[2304]{0:T(1024)(128)(2,1)} %get-tuple-element.15, ...), channel_id=2, replica_groups=mesh['dp'=8,'tensor'=4] {'dp'}, use_global_device_ids=true, to_apply=%region_18.19.clone | all-reduce | flops 9216 | bytes 36864
  1058.3 1.4 dynamic-slice_convert_fusion.2
  1059.7 1.4 dynamic-slice_convert_fusion
  1061.7 4.8 fusion.16
  1066.6 17.3 reduce-scatter.10.cloned.1.call-done
  1083.8 1.6 convert_element_type.194
  1085.5 65.6 %reduce-scatter.12.cloned.1.call-done = bf16[288,256]{1,0:T(8,128)(2,1)} async-done(((bf16[2304,256]{1,0:T(8,128)(2,1)}), bf16[288,256]{1,0:T(8,128)(2,1)}) %reduce-scatter.12.cloned.1.call-update) | async-done | bytes 147472 | tf_op jit(solution)/shard_map/reduce_scatter | solution.py:207
  1151.1 1.6 convert_element_type.196
  1152.7 70.9 %reduce-scatter.8.cloned.1.call-done = bf16[288,512]{1,0:T(8,128)(2,1)} async-done(((bf16[2304,512]{1,0:T(8,128)(2,1)}), bf16[288,512]{1,0:T(8,128)(2,1)}) %reduce-scatter.8.cloned.1.call-update) | async-done | bytes 294928 | tf_op jit(solution)/shard_map/reduce_scatter | solution.py:201
  1223.7 1.8 convert_element_type.192
  1225.5 70.9 %reduce-scatter.14.cloned.1.call-done = bf16[512,288]{0,1:T(8,128)(2,1)} async-done(((bf16[512,2304]{0,1:T(8,128)(2,1)}), bf16[512,288]{0,1:T(8,128)(2,1)}) %reduce-scatter.14.cloned.1.call-update) | async-done | bytes 294928 | tf_op jit(solution)/shard_map/reduce_scatter | solution.py:210
  1296.4 1.8 convert_element_type.198
  1298.2 180.9 %reduce-scatter.16.cloned.1.call-done = bf16[288,2304]{1,0:T(8,128)(2,1)} async-done(((bf16[2304,2304]{1,0:T(8,128)(2,1)}), bf16[288,2304]{1,0:T(8,128)(2,1)}) %reduce-scatter.16.cloned.1.call-update) | async-done | bytes 1327120 | tf_op jit(solution)/shard_map/reduce_scatter | solution.py:219
  1479.2 3.0 convert_element_type.204
  1482.2 179.6 %reduce-scatter.18.cloned.1.call-done = bf16[288,2304]{1,0:T(8,128)(2,1)} async-done(((bf16[2304,2304]{1,0:T(8,128)(2,1)}), bf16[288,2304]{1,0:T(8,128)(2,1)}) %reduce-scatter.18.cloned.1.call-update) | async-done | bytes 1327120 | tf_op jit(solution)/shard_map/reduce_scatter | solution.py:222
  1661.8 3.0 convert_element_type.206
  1664.8 179.7 %reduce-scatter.20.cloned.1.call-done = bf16[2304,288]{0,1:T(8,128)(2,1)} async-done(((bf16[2304,2304]{0,1:T(8,128)(2,1)}), bf16[2304,288]{0,1:T(8,128)(2,1)}) %reduce-scatter.20.cloned.1.call-update) | async-done | bytes 1327120 | tf_op jit(solution)/shard_map/reduce_scatter | solution.py:225
  1844.5 3.0 convert_element_type.208
  (189 shorter events, 25.0 us)
Async XLA Ops:
  7.2 46.9 %all-gather.10.cloned.1.call-start = ((), (), s32[]{:S(2)}) async-start(), calls=%async_computation.8 | async-start | bytes 1327104 | tf_op jit(solution)/shard_map/all_gather | solution.py:85
  7.9 88.2 %all-gather.12.cloned.1.call-start = ((), (), s32[]{:S(2)}) async-start(), calls=%async_computation.9 | async-start | bytes 1327104 | tf_op jit(solution)/shard_map/all_gather | solution.py:86
  8.7 140.1 %all-gather.8.cloned.1.call-start = ((), (), s32[]{:S(2)}) async-start(), calls=%async_computation.7 | async-start | bytes 2654208 | tf_op jit(solution)/shard_map/all_gather | solution.py:84
  9.4 191.8 %all-gather.14.cloned.1.call-start = ((), (), s32[]{:S(2)}) async-start(), calls=%async_computation.10 | async-start | bytes 2654208 | tf_op jit(solution)/shard_map/all_gather | solution.py:87
  10.0 269.4 %all-reduce.10.cloned.1.call-start = ((), (), s32[]{:S(2)}) async-start(), calls=%async_computation.11 | async-start | bytes 7077888 | tf_op jit(solution)/shard_map/psum | solution.py:121
  14.1 134.7 %copy-start.50 = (f32[384]{0:T(512)}, f32[384]{0:T(512)S(1)}, u32[]{:S(2)}) copy-start(f32[384]{0:T(512)S(1)} %fusion.69) | copy-start | bytes 4612
  14.9 138.5 %copy-start.33 = (pred[384,384]{0,1:T(8,128)(4,1)}, pred[384,384]{0,1:T(8,128)(4,1)S(1)}, u32[]{:S(2)}) copy-start(pred[384,384]{0,1:T(8,128)(4,1)S(1)} %fusion.50) | copy-start | bytes 442372
  15.7 41.2 %copy-start.17 = (f32[384,128]{0,1:T(8,128)}, f32[384,128]{0,1:T(8,128)S(1)}, u32[]{:S(2)}) copy-start(f32[384,128]{0,1:T(8,128)S(1)} %get-tuple-element.44) | copy-start | bytes 589828
  15.7 41.2 %copy-start.19 = (f32[384,128]{0,1:T(8,128)}, f32[384,128]{0,1:T(8,128)S(1)}, u32[]{:S(2)}) copy-start(f32[384,128]{0,1:T(8,128)S(1)} %get-tuple-element.45) | copy-start | bytes 589828
  15.7 80.3 %copy-start.4 = (bf16[384,2304]{1,0:T(8,128)(2,1)S(1)}, bf16[384,2304]{1,0:T(8,128)(2,1)}, u32[]{:S(2)}) copy-start(bf16[384,2304]{1,0:T(8,128)(2,1)} %param.14) | copy-start | bytes 5308420
  15.7 80.3 %copy-start.37 = (f32[2304]{0:T(1024)S(1)}, f32[2304]{0:T(1024)}, u32[]{:S(2)}) copy-start(f32[2304]{0:T(1024)} %param.17) | copy-start | bytes 27652
  56.9 95.1 %copy-start.10 = (f32[384,256]{0,1:T(8,128)}, f32[384,256]{0,1:T(8,128)S(1)}, u32[]{:S(2)}) copy-start(f32[384,256]{0,1:T(8,128)S(1)} %get-tuple-element.42) | copy-start | bytes 1179652
  57.0 95.1 %copy-start.12 = (f32[384,256]{0,1:T(8,128)}, f32[384,256]{0,1:T(8,128)S(1)}, u32[]{:S(2)}) copy-start(f32[384,256]{0,1:T(8,128)S(1)} %get-tuple-element.43) | copy-start | bytes 1179652
  57.0 95.3 %copy-start.27 = (bf16[384,256,1]{0,1,2:T(8,128)(2,1)}, bf16[384,256,1]{0,1,2:T(8,128)(2,1)S(1)}, u32[]{:S(2)}) copy-start(bf16[384,256,1]{0,1,2:T(8,128)(2,1)S(1)} %get-tuple-element.41) | copy-start | bytes 589828
  98.0 55.4 %copy-start.31 = (bf16[384,256,1]{1,0,2:T(8,128)(2,1)}, bf16[384,256,1]{1,0,2:T(8,128)(2,1)S(1)}, u32[]{:S(2)}) copy-start(bf16[384,256,1]{1,0,2:T(8,128)(2,1)S(1)} %fusion.31) | copy-start | bytes 589828
  153.4 52.4 %copy-start.25 = (f32[2,384,384]{1,2,0:T(8,128)}, f32[2,384,384]{1,2,0:T(8,128)S(1)}, u32[]{:S(2)}) copy-start(f32[2,384,384]{1,2,0:T(8,128)S(1)} %fusion.20) | copy-start | bytes 3538948
  154.2 51.6 %copy-start.29 = (bf16[2,384,256]{1,2,0:T(8,128)(2,1)}, bf16[2,384,256]{1,2,0:T(8,128)(2,1)S(1)}, u32[]{:S(2)}) copy-start(bf16[2,384,256]{1,2,0:T(8,128)(2,1)S(1)} %convolution_convert_fusion.8) | copy-start | bytes 1179652
  205.8 76.6 %copy-start.34 = (f32[2304]{0:T(1024)S(1)}, f32[2304]{0:T(1024)}, u32[]{:S(2)}) copy-start(f32[2304]{0:T(1024)} %param.22) | copy-start | bytes 27652
  205.8 227.8 %all-gather.16.cloned.1.call-start = ((), (), s32[]{:S(2)}) async-start(), calls=%async_computation.12 | async-start | bytes 11943936 | tf_op jit(solution)/shard_map/all_gather | solution.py:88
  206.4 379.8 %all-gather.18.cloned.1.call-start = ((), (), s32[]{:S(2)}) async-start(), calls=%async_computation.13 | async-start | bytes 11943936 | tf_op jit(solution)/shard_map/all_gather | solution.py:89
  207.2 531.5 %all-gather.20.cloned.1.call-start = ((), (), s32[]{:S(2)}) async-start(), calls=%async_computation.14 | async-start | bytes 11943936 | tf_op jit(solution)/shard_map/all_gather | solution.py:90
  207.9 614.6 %all-reduce.12.cloned.1.call-start = ((), (), s32[]{:S(2)}) async-start(), calls=%async_computation.15 | async-start | bytes 7077888 | tf_op jit(solution)/shard_map/psum | solution.py:128
  279.4 3.1 copy-start
  282.4 3.5 copy-start.35
  749.3 190.2 %all-reduce.14.cloned.1.call-start = ((), (), s32[]{:S(2)}) async-start(), calls=%async_computation.16 | async-start | bytes 7077888 | tf_op jit(solution)/shard_map/psum | solution.py:142
  822.5 3.1 copy-start.7
  822.5 3.1 copy-start.41
  825.6 5.0 copy-start.53
  825.6 5.0 copy-start.9
  825.6 5.0 copy-start.52
  825.6 5.0 copy-start.55
  825.6 18.2 slice-start
  830.6 13.2 copy-start.54
  830.6 13.2 slice-start.1
  830.6 13.2 slice-start.2
  843.8 7.7 copy-start.56
  864.5 151.3 %all-reduce.16.cloned.1.call-start = ((), (), s32[]{:S(2)}) async-start(), calls=%async_computation.17 | async-start | bytes 3538944 | tf_op jit(solution)/shard_map/psum | solution.py:193
  939.6 3.7 copy-start.47
  939.6 3.7 copy-start.1
  939.6 4.2 copy-start.6
  939.6 4.2 copy-start.36
  939.6 4.2 copy-start.40
  939.6 4.2 copy-start.42
  943.8 4.1 copy-start.45
  947.9 3.4 copy-start.15
  951.4 2.6 copy-start.28
  952.4 4.8 copy-start.23
  957.3 6.0 copy-start.11
  957.3 6.0 copy-start.13
  960.6 2.9 copy-start.18
  960.6 2.9 copy-start.20
  969.3 114.5 %reduce-scatter.10.cloned.1.call-start = ((), (), s32[]{:S(2)}) async-start(), calls=%async_computation.19 | async-start | bytes 1327104 | tf_op jit(solution)/shard_map/reduce_scatter | solution.py:204
  971.4 179.7 %reduce-scatter.12.cloned.1.call-start = ((), (), s32[]{:S(2)}) async-start(), calls=%async_computation.20 | async-start | bytes 1327104 | tf_op jit(solution)/shard_map/reduce_scatter | solution.py:207
  973.5 3.3 copy-start.30
  973.5 250.2 %reduce-scatter.8.cloned.1.call-start = ((), (), s32[]{:S(2)}) async-start(), calls=%async_computation.18 | async-start | bytes 2654208 | tf_op jit(solution)/shard_map/reduce_scatter | solution.py:201
  976.7 4.6 copy-start.16
  976.7 319.7 %reduce-scatter.14.cloned.1.call-start = ((), (), s32[]{:S(2)}) async-start(), calls=%async_computation.21 | async-start | bytes 2654208 | tf_op jit(solution)/shard_map/reduce_scatter | solution.py:210
  981.3 497.9 %reduce-scatter.16.cloned.1.call-start = ((), (), s32[]{:S(2)}) async-start(), calls=%async_computation.22 | async-start | bytes 11943936 | tf_op jit(solution)/shard_map/reduce_scatter | solution.py:219
  991.2 670.6 %reduce-scatter.18.cloned.1.call-start = ((), (), s32[]{:S(2)}) async-start(), calls=%async_computation.23 | async-start | bytes 11943936 | tf_op jit(solution)/shard_map/reduce_scatter | solution.py:222
  1000.9 2.1 copy-start.8
  1001.0 2.1 copy-start.43
  1001.0 843.5 %reduce-scatter.20.cloned.1.call-start = ((), (), s32[]{:S(2)}) async-start(), calls=%async_computation.24 | async-start | bytes 11943936 | tf_op jit(solution)/shard_map/reduce_scatter | solution.py:225
  1013.7 47.3 %copy-start.49 = (f32[384]{0:T(512)S(1)}, f32[384]{0:T(512)}, u32[]{:S(2)}) copy-start(f32[384]{0:T(512)} %copy-done.48) | copy-start | bytes 4612
  1013.7 48.0 %copy-start.3 = (f32[384,2304]{1,0:T(8,128)S(1)}, f32[384,2304]{1,0:T(8,128)}, u32[]{:S(2)}) copy-start(f32[384,2304]{1,0:T(8,128)} %copy-done.2) | copy-start | bytes 10616836
  (15 other events, 19.3 us)
Sparse Core Ops, SparseCore 0:
  10.2 43.8 all-gather.9
  56.2 39.7 all-gather.11
  98.3 50.4 all-gather.7
  150.8 50.3 all-gather.13
  206.0 73.3 all-reduce.9
  281.4 152.2 all-gather.15
  435.8 150.2 all-gather.17
  588.4 150.2 all-gather.19
  749.5 72.9 all-reduce.11
  864.6 74.9 all-reduce.13
  969.4 46.1 all-reduce.15
  1018.9 64.8 reduce-scatter.9
  1087.2 63.8 reduce-scatter.11
  1155.0 68.6 reduce-scatter.7
  1227.6 68.7 reduce-scatter.13
  1299.9 179.2 reduce-scatter.15
  1482.6 179.1 reduce-scatter.17
  1665.3 179.1 reduce-scatter.19
where the time goes:
time: 1860 us; the launch traced here: 1850 us
  waiting for transfers between devices  1590 us (85%)
  matrix products  137 us (7%)
  other arithmetic  61 us (3%)
  blocking collectives  38.6 us (2%)
    reduce_scatter x1, waiting for transfers between devices, shards(): lax.psum_scatter(grad_w_gate.astype(jnp.bfloat16), 'dp', scatter_dimensio...  181 us
    reduce_scatter x1, waiting for transfers between devices, shards(): lax.psum_scatter(grad_w_down.astype(jnp.bfloat16), 'dp', scatter_dimensio...  180 us
    reduce_scatter x1, waiting for transfers between devices, shards(): lax.psum_scatter(grad_w_up.astype(jnp.bfloat16), 'dp', scatter_dimension=...  180 us
    all_gather x1, waiting for transfers between devices, shards(): lax.all_gather(w_gate, 'dp', axis=0, tiled=True)  146 us
    all_gather x1, waiting for transfers between devices, shards(): lax.all_gather(w_up, 'dp', axis=0, tiled=True)  142 us
    all_gather x1, waiting for transfers between devices, shards(): lax.all_gather(w_down, 'dp', axis=1, tiled=True)  140 us
    psum x1, waiting for transfers between devices, shards(): ffn_branch = lax.psum(matmul(hidden, down_full), 'tensor')  71.7 us
    psum x1, waiting for transfers between devices, shards(): attn_branch = lax.psum(matmul(mixed_flat, out_full), 'tensor')  71.2 us
  transfers between devices with their start and end apart: 18, of which 17 were waited for; matrix products, arithmetic and copies ran while one was open for 6% of the time, Pallas kernels for 0%

commit v1 on v0

--- a/solution.py
+++ b/solution.py
@@ -11,6 +11,19 @@
 SOFT_CAP = 50.0
 QUERY_SCALE = 0.0625
 GELU_COEFF = 0.7978845608028654
+
+
+def ring_gather(shard, axis, dim):
+    ways = lax.axis_size(axis)
+    up = [(d, (d + 1) % ways) for d in range(ways)]
+    down = [(d, (d - 1) % ways) for d in range(ways)]
+    earlier, later = ([shard], [shard])
+    for _ in range(ways // 2):
+        earlier.append(lax.ppermute(earlier[-1], axis, up))
+    for _ in range((ways - 1) // 2):
+        later.append(lax.ppermute(later[-1], axis, down))
+    line = jnp.concatenate([*earlier[::-1], *later[1:]], axis=dim)
+    return jnp.roll(line, (lax.axis_index(axis) - ways // 2) * shard.shape[dim], axis=dim)
 
 
 def rms_scale(values, scales):
@@ -86,7 +99,7 @@
         lax.all_gather(w_value, "dp", axis=0, tiled=True),
         lax.all_gather(w_out, "dp", axis=1, tiled=True),
         lax.all_gather(w_gate, "dp", axis=0, tiled=True),
-        lax.all_gather(w_up, "dp", axis=0, tiled=True),
+        ring_gather(w_up, "dp", 0),
         lax.all_gather(w_down, "dp", axis=1, tiled=True),
     )
     query_full, key_full, value_full, out_full, gate_full, up_full, down_full = gathered

time: 1860 us -> 1790 us (0.962)
  waiting for transfers between devices: 1590 us -> 1470 us
  local copies, waits for them, and re-layouts: 13.6 us -> 44.8 us
    ppermute x0 -> x7, waiting for transfers between devices: none -> 230 us  [the longest x4 226 us: ring_gather(): earlier.append(lax.ppermute(earlier[-1], axis, up))]
    all_gather x1 -> x0, waiting for transfers between devices: 142 us -> none  [shards(): lax.all_gather(w_up, 'dp', axis=0, tiled=True)]
    all_gather x1, waiting for transfers between devices: 146 us -> 26 us  [shards(): lax.all_gather(w_gate, 'dp', axis=0, tiled=True)]
    psum x1, waiting for transfers between devices: 71.2 us -> 0.01 us  [shards(): attn_branch = lax.psum(matmul(mixed_flat, out_full), 'tensor')]
    unnamed x123 -> x148, local copies, waits for them, and re-layouts: 12.9 us -> 43 us
  transfers between devices with their start and end apart: 18 -> 24, of which waited for: 17 -> 20; matrix products, arithmetic and copies ran while one was open for 6% -> 8% of each run, Pallas kernels for 0% -> 0%
where the time goes in v1:
time: 1790 us; the launch traced here: 1780 us
  waiting for transfers between devices  1470 us (82%)
  matrix products  136 us (8%)
  other arithmetic  61 us (3%)
  local copies, waits for them, and re-layouts  44.8 us (3%)
  blocking collectives  38.6 us (2%)
    ppermute x4, waiting for transfers between devices, ring_gather(): earlier.append(lax.ppermute(earlier[-1], axis, up))  226 us
    reduce_scatter x1, waiting for transfers between devices, shards(): lax.psum_scatter(grad_w_gate.astype(jnp.bfloat16), 'dp', scatter_dimensio...  181 us
    reduce_scatter x1, waiting for transfers between devices, shards(): lax.psum_scatter(grad_w_up.astype(jnp.bfloat16), 'dp', scatter_dimension=...  180 us
    reduce_scatter x1, waiting for transfers between devices, shards(): lax.psum_scatter(grad_w_down.astype(jnp.bfloat16), 'dp', scatter_dimensio...  180 us
    all_gather x1, waiting for transfers between devices, shards(): lax.all_gather(w_down, 'dp', axis=1, tiled=True)  129 us
    psum x1, waiting for transfers between devices, shards(): ffn_branch = lax.psum(matmul(hidden, down_full), 'tensor')  71.5 us
    psum x1, waiting for transfers between devices, shards(): lax.psum(right_product(grad_gate, gate_back) + right_product(grad_up, up_...  71.3 us
    reduce_scatter x1, waiting for transfers between devices, shards(): lax.psum_scatter(grad_w_out.astype(jnp.bfloat16), 'dp', scatter_dimension...  71.1 us
  transfers between devices with their start and end apart: 24, of which 20 were waited for; matrix products, arithmetic and copies ran while one was open for 8% of the time, Pallas kernels for 0%

profile of v1, /device:TPU:0, one launch (start us, length us, event | category | flops | bytes accessed | tf_op | source)
XLA Modules:
  0.0 1782.9 jit_solution(4717562857470577595)
XLA Ops:
  15.7 38.3 %all-gather.9.cloned.1.call-done = bf16[2304,256]{1,0:T(8,128)(2,1)} async-done(((bf16[288,256]{1,0:T(8,128)(2,1)}), bf16[2304,256]{1,0:T(8,128)(2,1)}) %all-gather.9.cloned.1.call-update) | async-done | bytes 1179664 | tf_op jit(solution)/shard_map/all_gather | solution.py:98
  54.0 2.7 fusion.103
  57.0 39.1 %all-gather.11.cloned.1.call-done = bf16[2304,256]{1,0:T(8,128)(2,1)} async-done(((bf16[288,256]{1,0:T(8,128)(2,1)}), bf16[2304,256]{1,0:T(8,128)(2,1)}) %all-gather.11.cloned.1.call-update) | async-done | bytes 1179664 | tf_op jit(solution)/shard_map/all_gather | solution.py:99
  98.0 50.8 %all-gather.7.cloned.1.call-done = bf16[2304,512]{1,0:T(8,128)(2,1)} async-done(((bf16[288,512]{1,0:T(8,128)(2,1)}), bf16[2304,512]{1,0:T(8,128)(2,1)}) %all-gather.7.cloned.1.call-update) | async-done | bytes 2359312 | tf_op jit(solution)/shard_map/all_gather | solution.py:97
  148.8 3.2 fusion.105
  154.2 47.0 %all-gather.13.cloned.1.call-done = bf16[512,2304]{0,1:T(8,128)(2,1)} async-done(((bf16[512,288]{0,1:T(8,128)(2,1)}), bf16[512,2304]{0,1:T(8,128)(2,1)}) %all-gather.13.cloned.1.call-update) | async-done | bytes 2359312 | tf_op jit(solution)/shard_map/all_gather | solution.py:100
  201.2 4.6 fusion.108
  207.8 31.5 %collective-permute-done = bf16[288,2304]{1,0:T(8,128)(2,1)S(1)} collective-permute-done((bf16[288,2304]{1,0:T(8,128)(2,1)S(1)}, bf16[288,2304]{1,0:T(8,128)(2,1)S(1)}, u32[]{:S(2)}, u32[]{:S(2)}) %collective-permute-start) | collective-permute-done | bytes 1327136 | tf_op jit(solution)/shard_map/ppermute | solution.py:22
  239.3 4.7 collective-permute-start.4
  244.1 57.1 %collective-permute-done.1 = bf16[288,2304]{1,0:T(8,128)(2,1)S(1)} collective-permute-done((bf16[288,2304]{1,0:T(8,128)(2,1)S(1)}, bf16[288,2304]{1,0:T(8,128)(2,1)S(1)}, u32[]{:S(2)}, u32[]{:S(2)}) %collective-permute-start.1) | collective-permute-done | bytes 1327136 | tf_op jit(solution)/shard_map/ppermute | solution.py:22
  301.2 2.5 collective-permute-start.2
  303.6 3.2 collective-permute-done.4
  306.9 58.3 %collective-permute-done.2 = bf16[288,2304]{1,0:T(8,128)(2,1)} collective-permute-done((bf16[288,2304]{1,0:T(8,128)(2,1)S(1)}, bf16[288,2304]{1,0:T(8,128)(2,1)}, u32[]{:S(2)}, u32[]{:S(2)}) %collective-permute-start.2) | collective-permute-done | bytes 1327136 | tf_op jit(solution)/shard_map/ppermute | solution.py:22
  365.2 2.6 collective-permute-start.3
  367.8 2.3 collective-permute-start.6
  370.1 79.5 %collective-permute-done.3 = bf16[288,2304]{1,0:T(8,128)(2,1)} collective-permute-done((bf16[288,2304]{1,0:T(8,128)(2,1)}, bf16[288,2304]{1,0:T(8,128)(2,1)}, u32[]{:S(2)}, u32[]{:S(2)}) %collective-permute-start.3) | collective-permute-done | bytes 1327136 | tf_op jit(solution)/shard_map/ppermute | solution.py:22
  449.6 2.5 constant_dynamic-update-slice_fusion.15
  452.1 2.5 constant_dynamic-update-slice_fusion.14
  458.2 2.5 constant_dynamic-update-slice_fusion.10
  460.7 2.5 constant_dynamic-update-slice_fusion.9
  464.4 2.5 constant_dynamic-update-slice_fusion.7
  466.9 2.5 constant_dynamic-update-slice_fusion.6
  472.9 2.5 constant_dynamic-update-slice_fusion.2
  475.4 2.5 constant_dynamic-update-slice_fusion.1
  479.1 2.5 multiply_reduce_fusion.8
  482.2 2.4 multiply_reduce_fusion.7
  487.3 26.0 %all-gather.15.cloned.1.call-done = bf16[2304,2304]{1,0:T(8,128)(2,1)} async-done(((bf16[288,2304]{1,0:T(8,128)(2,1)}), bf16[2304,2304]{1,0:T(8,128)(2,1)}) %all-gather.15.cloned.1.call-update) | async-done | bytes 10616848 | tf_op jit(solution)/shard_map/all_gather | solution.py:101
  513.2 9.3 fusion.109
  524.3 12.7 multiply_convert_fusion.1
  537.0 129.2 %all-gather.17.cloned.1.call-done = bf16[2304,2304]{0,1:T(8,128)(2,1)} async-done(((bf16[2304,288]{0,1:T(8,128)(2,1)}), bf16[2304,2304]{0,1:T(8,128)(2,1)}) %all-gather.17.cloned.1.call-update) | async-done | bytes 10616848 | tf_op jit(solution)/shard_map/all_gather | solution.py:103
  666.2 10.6 fusion.110
  678.6 71.5 %all-reduce.12.cloned.1.call-done = f32[384,2304]{1,0:T(8,128)} async-done(((f32[384,2304]{1,0:T(8,128)}), f32[384,2304]{1,0:T(8,128)}) %all-reduce.12.cloned.1.call-update) | async-done | bytes 3538960 | tf_op jit(solution)/shard_map/psum | solution.py:141
  750.1 2.5 multiply_reduce_fusion.6
  753.2 5.0 multiply_reduce_fusion
  758.2 13.2 multiply_convert_fusion
  771.4 7.7 fusion.111
  779.1 13.2 fusion.6
  792.6 3.5 fusion.31
  796.1 71.3 %all-reduce.14.cloned.1.call-done = f32[384,2304]{1,0:T(8,128)} async-done(((f32[384,2304]{1,0:T(8,128)}), f32[384,2304]{1,0:T(8,128)}) %all-reduce.14.cloned.1.call-update) | async-done | bytes 3538960 | tf_op jit(solution)/shard_map/psum | solution.py:155
  867.5 3.7 multiply_reduce_fusion.1
  871.7 4.1 multiply_reduce_fusion.2
  881.9 3.4 fusion.44
  885.3 3.4 fusion.41
  888.7 2.6 fusion.37
  897.5 2.0 convolution_convert_fusion.6
  899.5 2.0 convolution_convert_fusion.5
  901.9 3.0 convolution_convert_fusion.4
  904.9 4.4 convolution_convert_fusion.3
  909.5 9.9 convolution_convert_fusion.2
  920.9 8.3 convolution_convert_fusion.1
  931.2 10.7 convolution_convert_fusion
  943.9 3.9 fusion.13
  947.9 38.6 %all-reduce.4 = (bf16[2304]{0:T(1024)(128)(2,1)}, bf16[2304]{0:T(1024)(128)(2,1)}, bf16[2304]{0:T(1024)(128)(2,1)}, bf16[2304]{0:T(1024)(128)(2,1)}) all-reduce(bf16[2304]{0:T(1024)(128)(2,1)} %get-tuple-element.19, bf16[2304]{0:T(1024)(128)(2,1)} %get-tuple-element.15, ...), channel_id=2, replica_groups=mesh['dp'=8,'tensor'=4] {'dp'}, use_global_device_ids=true, to_apply=%region_18.19.clone | all-reduce | flops 9216 | bytes 36864
  989.9 4.8 fusion.23
  994.7 17.3 reduce-scatter.10.cloned.1.call-done
  1013.6 65.5 %reduce-scatter.12.cloned.1.call-done = bf16[288,256]{1,0:T(8,128)(2,1)} async-done(((bf16[2304,256]{1,0:T(8,128)(2,1)}), bf16[288,256]{1,0:T(8,128)(2,1)}) %reduce-scatter.12.cloned.1.call-update) | async-done | bytes 147472 | tf_op jit(solution)/shard_map/reduce_scatter | solution.py:220
  1080.8 71.1 %reduce-scatter.8.cloned.1.call-done = bf16[288,512]{1,0:T(8,128)(2,1)} async-done(((bf16[2304,512]{1,0:T(8,128)(2,1)}), bf16[288,512]{1,0:T(8,128)(2,1)}) %reduce-scatter.8.cloned.1.call-update) | async-done | bytes 294928 | tf_op jit(solution)/shard_map/reduce_scatter | solution.py:214
  1153.7 71.1 %reduce-scatter.14.cloned.1.call-done = bf16[512,288]{0,1:T(8,128)(2,1)} async-done(((bf16[512,2304]{0,1:T(8,128)(2,1)}), bf16[512,288]{0,1:T(8,128)(2,1)}) %reduce-scatter.14.cloned.1.call-update) | async-done | bytes 294928 | tf_op jit(solution)/shard_map/reduce_scatter | solution.py:223
  1226.7 180.9 %reduce-scatter.16.cloned.1.call-done = bf16[288,2304]{1,0:T(8,128)(2,1)} async-done(((bf16[2304,2304]{1,0:T(8,128)(2,1)}), bf16[288,2304]{1,0:T(8,128)(2,1)}) %reduce-scatter.16.cloned.1.call-update) | async-done | bytes 1327120 | tf_op jit(solution)/shard_map/reduce_scatter | solution.py:232
  1407.6 3.0 convert_element_type.204
  1410.6 179.7 %reduce-scatter.18.cloned.1.call-done = bf16[288,2304]{1,0:T(8,128)(2,1)} async-done(((bf16[2304,2304]{1,0:T(8,128)(2,1)}), bf16[288,2304]{1,0:T(8,128)(2,1)}) %reduce-scatter.18.cloned.1.call-update) | async-done | bytes 1327120 | tf_op jit(solution)/shard_map/reduce_scatter | solution.py:235
  1590.3 3.0 convert_element_type.206
  1593.3 179.6 %reduce-scatter.20.cloned.1.call-done = bf16[2304,288]{0,1:T(8,128)(2,1)} async-done(((bf16[2304,2304]{0,1:T(8,128)(2,1)}), bf16[2304,288]{0,1:T(8,128)(2,1)}) %reduce-scatter.20.cloned.1.call-update) | async-done | bytes 1327120 | tf_op jit(solution)/shard_map/reduce_scatter | solution.py:238
  1772.9 3.0 convert_element_type.208
  (226 shorter events, 60.2 us)
Async XLA Ops:
  7.2 46.9 %all-gather.9.cloned.1.call-start = ((), (), s32[]{:S(2)}) async-start(), calls=%async_computation.8 | async-start | bytes 1327104 | tf_op jit(solution)/shard_map/all_gather | solution.py:98
  7.9 88.2 %all-gather.11.cloned.1.call-start = ((), (), s32[]{:S(2)}) async-start(), calls=%async_computation.9 | async-start | bytes 1327104 | tf_op jit(solution)/shard_map/all_gather | solution.py:99
  8.7 140.1 %all-gather.7.cloned.1.call-start = ((), (), s32[]{:S(2)}) async-start(), calls=%async_computation.7 | async-start | bytes 2654208 | tf_op jit(solution)/shard_map/all_gather | solution.py:97
  9.4 191.8 %all-gather.13.cloned.1.call-start = ((), (), s32[]{:S(2)}) async-start(), calls=%async_computation.10 | async-start | bytes 2654208 | tf_op jit(solution)/shard_map/all_gather | solution.py:100
  10.0 469.1 %all-reduce.10.cloned.1.call-start = ((), (), s32[]{:S(2)}) async-start(), calls=%async_computation.11 | async-start | bytes 7077888 | tf_op jit(solution)/shard_map/psum | solution.py:134
  14.1 134.7 %copy-start.54 = (f32[384]{0:T(512)}, f32[384]{0:T(512)S(1)}, u32[]{:S(2)}) copy-start(f32[384]{0:T(512)S(1)} %fusion.76) | copy-start | bytes 4612
  14.9 138.5 %copy-start.37 = (pred[384,384]{0,1:T(8,128)(4,1)}, pred[384,384]{0,1:T(8,128)(4,1)S(1)}, u32[]{:S(2)}) copy-start(pred[384,384]{0,1:T(8,128)(4,1)S(1)} %fusion.57) | copy-start | bytes 442372
  15.7 41.2 %copy-start.21 = (f32[384,128]{0,1:T(8,128)}, f32[384,128]{0,1:T(8,128)S(1)}, u32[]{:S(2)}) copy-start(f32[384,128]{0,1:T(8,128)S(1)} %get-tuple-element.44) | copy-start | bytes 589828
  15.7 41.2 %copy-start.23 = (f32[384,128]{0,1:T(8,128)}, f32[384,128]{0,1:T(8,128)S(1)}, u32[]{:S(2)}) copy-start(f32[384,128]{0,1:T(8,128)S(1)} %get-tuple-element.45) | copy-start | bytes 589828
  15.7 80.3 %copy-start.4 = (bf16[384,2304]{1,0:T(8,128)(2,1)S(1)}, bf16[384,2304]{1,0:T(8,128)(2,1)}, u32[]{:S(2)}) copy-start(bf16[384,2304]{1,0:T(8,128)(2,1)} %param.14) | copy-start | bytes 5308420
  15.7 80.3 %copy-start.41 = (f32[2304]{0:T(1024)S(1)}, f32[2304]{0:T(1024)}, u32[]{:S(2)}) copy-start(f32[2304]{0:T(1024)} %param.17) | copy-start | bytes 27652
  56.9 95.1 %copy-start.13 = (f32[384,256]{0,1:T(8,128)}, f32[384,256]{0,1:T(8,128)S(1)}, u32[]{:S(2)}) copy-start(f32[384,256]{0,1:T(8,128)S(1)} %get-tuple-element.42) | copy-start | bytes 1179652
  57.0 95.1 %copy-start.15 = (f32[384,256]{0,1:T(8,128)}, f32[384,256]{0,1:T(8,128)S(1)}, u32[]{:S(2)}) copy-start(f32[384,256]{0,1:T(8,128)S(1)} %get-tuple-element.43) | copy-start | bytes 1179652
  57.0 95.3 %copy-start.31 = (bf16[384,256,1]{0,1,2:T(8,128)(2,1)}, bf16[384,256,1]{0,1,2:T(8,128)(2,1)S(1)}, u32[]{:S(2)}) copy-start(bf16[384,256,1]{0,1,2:T(8,128)(2,1)S(1)} %get-tuple-element.41) | copy-start | bytes 589828
  98.0 55.4 %copy-start.35 = (bf16[384,256,1]{1,0,2:T(8,128)(2,1)}, bf16[384,256,1]{1,0,2:T(8,128)(2,1)S(1)}, u32[]{:S(2)}) copy-start(bf16[384,256,1]{1,0,2:T(8,128)(2,1)S(1)} %fusion.38) | copy-start | bytes 589828
  153.4 47.8 %copy-start.29 = (f32[2,384,384]{1,2,0:T(8,128)}, f32[2,384,384]{1,2,0:T(8,128)S(1)}, u32[]{:S(2)}) copy-start(f32[2,384,384]{1,2,0:T(8,128)S(1)} %fusion.27) | copy-start | bytes 3538948
  154.2 47.0 %copy-start.33 = (bf16[2,384,256]{1,2,0:T(8,128)(2,1)}, bf16[2,384,256]{1,2,0:T(8,128)(2,1)S(1)}, u32[]{:S(2)}) copy-start(bf16[2,384,256]{1,2,0:T(8,128)(2,1)S(1)} %convolution_convert_fusion.8) | copy-start | bytes 1179652
  205.8 307.4 %all-gather.15.cloned.1.call-start = ((), (), s32[]{:S(2)}) async-start(), calls=%async_computation.12 | async-start | bytes 11943936 | tf_op jit(solution)/shard_map/all_gather | solution.py:101
  206.4 459.8 %all-gather.17.cloned.1.call-start = ((), (), s32[]{:S(2)}) async-start(), calls=%async_computation.13 | async-start | bytes 11943936 | tf_op jit(solution)/shard_map/all_gather | solution.py:103
  207.2 542.9 %all-reduce.12.cloned.1.call-start = ((), (), s32[]{:S(2)}) async-start(), calls=%async_computation.14 | async-start | bytes 7077888 | tf_op jit(solution)/shard_map/psum | solution.py:141
  207.2 32.1 %collective-permute-start = (bf16[288,2304]{1,0:T(8,128)(2,1)S(1)}, bf16[288,2304]{1,0:T(8,128)(2,1)S(1)}, u32[]{:S(2)}, u32[]{:S(2)}) collective-permute-start(bf16[288,2304]{1,0:T(8,128)(2,1)S(1)} %copy-done.10), channel_id=1, source_target_pairs={{0,4},{4,8},{8,12},{12,16},{16,20},{20,24},{24,28},{28,0},{1,5},{5... | collective-permute-start | bytes 3981320 | tf_op jit(solution)/shard_map/ppermute | solution.py:22
  239.3 61.8 %collective-permute-start.1 = (bf16[288,2304]{1,0:T(8,128)(2,1)S(1)}, bf16[288,2304]{1,0:T(8,128)(2,1)S(1)}, u32[]{:S(2)}, u32[]{:S(2)}) collective-permute-start(bf16[288,2304]{1,0:T(8,128)(2,1)S(1)} %collective-permute-done), channel_id=1, source_target_pairs={{0,4},{4,8},{8,12},{12,16},{16,20},{20,24},{24,28},{28,0},{1,5},{5... | collective-permute-start | bytes 3981320 | tf_op jit(solution)/shard_map/ppermute | solution.py:22
  239.3 67.5 %collective-permute-start.4 = (bf16[288,2304]{1,0:T(8,128)(2,1)S(1)}, bf16[288,2304]{1,0:T(8,128)(2,1)}, u32[]{:S(2)}, u32[]{:S(2)}) collective-permute-start(bf16[288,2304]{1,0:T(8,128)(2,1)S(1)} %copy-done.10), channel_id=1, source_target_pairs={{0,28},{4,0},{8,4},{12,8},{16,12},{20,16},{24,20},{28,24},{1,29},{... | collective-permute-start | bytes 3981320 | tf_op jit(solution)/shard_map/ppermute | solution.py:24
  301.2 5.7 copy-start.11
  301.2 64.0 %collective-permute-start.2 = (bf16[288,2304]{1,0:T(8,128)(2,1)S(1)}, bf16[288,2304]{1,0:T(8,128)(2,1)}, u32[]{:S(2)}, u32[]{:S(2)}) collective-permute-start(bf16[288,2304]{1,0:T(8,128)(2,1)S(1)} %collective-permute-done.1), channel_id=1, source_target_pairs={{0,4},{4,8},{8,12},{12,16},{16,20},{20,24},{24,28},{28,0},{1,5},{5... | collective-permute-start | bytes 3981320 | tf_op jit(solution)/shard_map/ppermute | solution.py:22
  306.8 60.9 %collective-permute-start.5 = (bf16[288,2304]{1,0:T(8,128)(2,1)}, bf16[288,2304]{1,0:T(8,128)(2,1)}, u32[]{:S(2)}, u32[]{:S(2)}) collective-permute-start(bf16[288,2304]{1,0:T(8,128)(2,1)} %collective-permute-done.4), channel_id=1, source_target_pairs={{0,28},{4,0},{8,4},{12,8},{16,12},{20,16},{24,20},{28,24},{1,29},{... | collective-permute-start | bytes 3981320 | tf_op jit(solution)/shard_map/ppermute | solution.py:24
  365.2 84.4 %collective-permute-start.3 = (bf16[288,2304]{1,0:T(8,128)(2,1)}, bf16[288,2304]{1,0:T(8,128)(2,1)}, u32[]{:S(2)}, u32[]{:S(2)}) collective-permute-start(bf16[288,2304]{1,0:T(8,128)(2,1)} %collective-permute-done.2), channel_id=1, source_target_pairs={{0,4},{4,8},{8,12},{12,16},{16,20},{20,24},{24,28},{28,0},{1,5},{5... | collective-permute-start | bytes 3981320 | tf_op jit(solution)/shard_map/ppermute | solution.py:22
  367.8 86.8 %copy-start.12 = (bf16[288,2304]{1,0:T(8,128)(2,1)S(1)}, bf16[288,2304]{1,0:T(8,128)(2,1)}, u32[]{:S(2)}) copy-start(bf16[288,2304]{1,0:T(8,128)(2,1)} %copy-done.11) | copy-start | bytes 3981316
  367.8 95.5 %collective-permute-start.6 = (bf16[288,2304]{1,0:T(8,128)(2,1)}, bf16[288,2304]{1,0:T(8,128)(2,1)S(1)}, u32[]{:S(2)}, u32[]{:S(2)}) collective-permute-start(bf16[288,2304]{1,0:T(8,128)(2,1)} %collective-permute-done.5), channel_id=1, source_target_pairs={{0,28},{4,0},{8,4},{12,8},{16,12},{20,16},{24,20},{28,24},{1,29},{... | collective-permute-start | bytes 3981320 | tf_op jit(solution)/shard_map/ppermute | solution.py:24
  477.9 4.2 copy-start.38
  482.2 3.5 copy-start.39
  513.2 11.1 copy-start.19
  676.9 190.6 %all-reduce.14.cloned.1.call-start = ((), (), s32[]{:S(2)}) async-start(), calls=%async_computation.15 | async-start | bytes 7077888 | tf_op jit(solution)/shard_map/psum | solution.py:155
  753.1 5.0 copy-start.57
  753.1 5.0 copy-start.9
  753.1 5.0 copy-start.56
  753.1 5.0 copy-start.60
  753.1 18.2 %slice-start = ((s8[10616832]{0:T(1024)(128)(4,1)}), s8[4194304]{0:T(1024)(128)(4,1)S(1)}, s32[]{:S(2)}) async-start(s8[10616832]{0:T(1024)(128)(4,1)} %bitcast.106), calls=%async_computation.24 | async-start | bytes 8388608
  758.1 13.2 copy-start.58
  758.2 13.2 slice-start.1
  758.2 13.2 slice-start.2
  771.4 7.7 copy-start.61
  792.4 151.5 %all-reduce.16.cloned.1.call-start = ((), (), s32[]{:S(2)}) async-start(), calls=%async_computation.16 | async-start | bytes 3538944 | tf_op jit(solution)/shard_map/psum | solution.py:206
  867.5 3.7 copy-start.51
  867.5 3.7 copy-start.1
  867.5 4.2 copy-start.6
  867.5 4.2 copy-start.40
  867.5 4.2 copy-start.44
  867.5 4.2 copy-start.46
  871.7 4.1 copy-start.49
  875.8 3.4 copy-start.18
  880.3 4.9 copy-start.27
  885.3 6.1 copy-start.14
  885.3 6.1 copy-start.16
  897.4 114.6 %reduce-scatter.10.cloned.1.call-start = ((), (), s32[]{:S(2)}) async-start(), calls=%async_computation.18 | async-start | bytes 1327104 | tf_op jit(solution)/shard_map/reduce_scatter | solution.py:217
  899.5 179.6 %reduce-scatter.12.cloned.1.call-start = ((), (), s32[]{:S(2)}) async-start(), calls=%async_computation.19 | async-start | bytes 1327104 | tf_op jit(solution)/shard_map/reduce_scatter | solution.py:220
  901.6 250.3 %reduce-scatter.8.cloned.1.call-start = ((), (), s32[]{:S(2)}) async-start(), calls=%async_computation.17 | async-start | bytes 2654208 | tf_op jit(solution)/shard_map/reduce_scatter | solution.py:214
  904.9 4.6 copy-start.20
  904.9 320.0 %reduce-scatter.14.cloned.1.call-start = ((), (), s32[]{:S(2)}) async-start(), calls=%async_computation.20 | async-start | bytes 2654208 | tf_op jit(solution)/shard_map/reduce_scatter | solution.py:223
  909.4 498.2 %reduce-scatter.16.cloned.1.call-start = ((), (), s32[]{:S(2)}) async-start(), calls=%async_computation.21 | async-start | bytes 11943936 | tf_op jit(solution)/shard_map/reduce_scatter | solution.py:232
  919.4 670.9 %reduce-scatter.18.cloned.1.call-start = ((), (), s32[]{:S(2)}) async-start(), calls=%async_computation.22 | async-start | bytes 11943936 | tf_op jit(solution)/shard_map/reduce_scatter | solution.py:235
  929.2 843.8 %reduce-scatter.20.cloned.1.call-start = ((), (), s32[]{:S(2)}) async-start(), calls=%async_computation.23 | async-start | bytes 11943936 | tf_op jit(solution)/shard_map/reduce_scatter | solution.py:238
  941.8 47.4 %copy-start.53 = (f32[384]{0:T(512)S(1)}, f32[384]{0:T(512)}, u32[]{:S(2)}) copy-start(f32[384]{0:T(512)} %copy-done.52) | copy-start | bytes 4612
  941.8 48.0 %copy-start.3 = (f32[384,2304]{1,0:T(8,128)S(1)}, f32[384,2304]{1,0:T(8,128)}, u32[]{:S(2)}) copy-start(f32[384,2304]{1,0:T(8,128)} %copy-done.2) | copy-start | bytes 10616836
  (26 other events, 47.6 us)
Sparse Core Ops, SparseCore 0:
  10.2 43.8 all-gather.8
  56.2 39.7 all-gather.10
  98.3 50.4 all-gather.6
  150.8 50.3 all-gather.12
  206.0 73.3 all-reduce.9
  281.4 231.7 all-gather.14
  515.4 150.7 all-gather.16
  677.0 72.9 all-reduce.11
  792.5 74.9 all-reduce.13
  897.5 46.1 all-reduce.15
  947.1 64.7 reduce-scatter.9
  1015.2 63.8 reduce-scatter.11
  1083.2 68.6 reduce-scatter.7
  1155.8 68.9 reduce-scatter.13
  1228.3 179.2 reduce-scatter.15
  1411.1 179.1 reduce-scatter.17
  1593.7 179.1 reduce-scatter.19
